TPU v7x, 256 devices: a whole 4x4x8 slice. The times are simulated.
256 devices in a mesh: unit: 4 (over z_hi), zero: 16 (over y, x), tp: 4 (over z_lo, core).
Axes of the slice: x: 4, y: 4, z: 8 (z_hi: 4, z_lo: 2; z = z_hi * 2 + z_lo), core: 2. Of those that a mesh axis runs over, the one named last changes fastest.
Arguments:
- weight_query: bfloat16 [16384, 4096], P(('unit', 'zero'), 'tp'), parts along dimension 0, may hold values from -0.125 to 0.125
- low_query: bfloat16 [16384, 32], P(('unit', 'zero')), parts along dimension 0, may hold values from -0.09375 to 0.09375
- high_query: bfloat16 [128, 4096], P('unit', 'tp'), parts along dimension 0, may hold values from -1 to 1
- weight_key: bfloat16 [16384, 1024], P(('unit', 'zero'), 'tp'), parts along dimension 0, may hold values from -0.125 to 0.125
- low_key: bfloat16 [16384, 32], P(('unit', 'zero')), parts along dimension 0, may hold values from -0.09375 to 0.09375
- high_key: bfloat16 [128, 1024], P('unit', 'tp'), parts along dimension 0, may hold values from -1 to 1
- weight_value: bfloat16 [16384, 1024], P(('unit', 'zero'), 'tp'), parts along dimension 0, may hold values from -0.125 to 0.125
- low_value: bfloat16 [16384, 32], P(('unit', 'zero')), parts along dimension 0, may hold values from -0.09375 to 0.09375
- high_value: bfloat16 [128, 1024], P('unit', 'tp'), parts along dimension 0, may hold values from -1 to 1
- norm_train: float32 [16384], P(('unit', 'zero', 'tp')), parts along dimension 0, may hold values from 0.25 to 1.75
- norm_step: float32 [16384], P(('unit', 'zero', 'tp')), parts along dimension 0, may hold values from -0.3 to 0.3
Outputs:
- serve_query: bfloat16 [16384, 4096], P('unit', 'tp'), parts along dimension 0
- serve_key: bfloat16 [16384, 1024], P('unit', 'tp'), parts along dimension 0
- serve_value: bfloat16 [16384, 1024], P('unit', 'tp'), parts along dimension 0
- column_query: float32 [16384], P(('unit', 'tp')), parts along dimension 0
- column_key: float32 [4096], P(('unit', 'tp')), parts along dimension 0
- column_value: float32 [4096], P(('unit', 'tp')), parts along dimension 0
- serve_norm: bfloat16 [16384], P('unit'), parts along dimension 0
There are 4 independent parts, one for each index of `unit`. A program takes and returns all parts, laid end to end along the dimension named above; each array names one. Nothing has to cross between parts.
All inputs are finite; a program needn't handle non-finite values.
Results may differ from a plain program's by a relative error of at most 0.001.
Values may be sent and summed in bfloat16 or wider, within the bound.
A program may use at most 64 MiB of HBM per device.

v0:
```python
import jax
import jax.numpy as jnp
from jax import lax
from jax.sharding import PartitionSpec as P

mix_rate = 2.0


def from_everyone(value, axis):
    copies = jnp.broadcast_to(value, (lax.axis_size(axis), *value.shape))
    return lax.all_to_all(copies, axis, split_axis=0, concat_axis=0, tiled=True)


def over_copies(value, axis):
    return from_everyone(value, axis).sum(axis=0)


def packed_total(arrays, axis):
    ends = [0]
    for a in arrays:
        ends.append(ends[-1] + a.size)
    running = over_copies(jnp.concatenate([a.ravel() for a in arrays]), axis)
    return tuple((running[b:e].reshape(a.shape) for a, b, e in zip(arrays, ends, ends[1:])))


def side_by_side(arrays, axis, dim, along):
    widths = [a.shape[along] for a in arrays]
    both = jnp.concatenate(arrays, axis=along)
    filled = lax.all_gather(both, axis, axis=dim, tiled=True)
    return tuple(jnp.split(filled, [sum(widths[:k]) for k in range(1, len(widths))], axis=along))


def laid_out(parts, dim):
    parts = jnp.moveaxis(parts, 0, dim)
    dims = parts.shape
    return parts.reshape(*dims[:dim], dims[dim] * dims[dim + 1], *dims[dim + 2 :])


def gathered_copies(value, axis, dim):
    return laid_out(from_everyone(value, axis), dim)


def on_device(
    weight_query,
    low_query,
    high_query,
    weight_key,
    low_key,
    high_key,
    weight_value,
    low_value,
    high_value,
    norm_train,
    norm_step,
):
    fresh_query = weight_query.astype(jnp.float32) + mix_rate * jnp.dot(
        low_query, high_query, preferred_element_type=jnp.float32
    )
    fresh_key = weight_key.astype(jnp.float32) + mix_rate * jnp.dot(
        low_key, high_key, preferred_element_type=jnp.float32
    )
    fresh_value = weight_value.astype(jnp.float32) + mix_rate * jnp.dot(
        low_value, high_value, preferred_element_type=jnp.float32
    )
    total_query, total_key, total_value = packed_total(
        (
            jnp.sum(fresh_query * fresh_query, axis=0),
            jnp.sum(fresh_key * fresh_key, axis=0),
            jnp.sum(fresh_value * fresh_value, axis=0),
        ),
        "zero",
    )
    column_query = jnp.sqrt(total_query)
    column_key = jnp.sqrt(total_key)
    column_value = jnp.sqrt(total_value)
    narrow_query, narrow_key, narrow_value = (
        (fresh_query / column_query).astype(jnp.bfloat16),
        (fresh_key / column_key).astype(jnp.bfloat16),
        (fresh_value / column_value).astype(jnp.bfloat16),
    )
    serve_query, serve_key, serve_value = side_by_side(
        (narrow_query, narrow_key, narrow_value), "zero", 0, 1
    )
    serve_norm = gathered_copies((norm_train + norm_step).astype(jnp.bfloat16), ("zero", "tp"), 0)
    return (serve_query, serve_key, serve_value, column_query, column_key, column_value, serve_norm)


def solution(mesh):
    placed = (
        P(("unit", "zero"), "tp"),
        P(("unit", "zero"), None),
        P("unit", "tp"),
        P(("unit", "zero"), "tp"),
        P(("unit", "zero"), None),
        P("unit", "tp"),
        P(("unit", "zero"), "tp"),
        P(("unit", "zero"), None),
        P("unit", "tp"),
        P(("unit", "zero", "tp")),
        P(("unit", "zero", "tp")),
    )
    return jax.shard_map(
        on_device,
        mesh=mesh,
        in_specs=placed,
        out_specs=(
            P("unit", "tp"),
            P("unit", "tp"),
            P("unit", "tp"),
            P(("unit", "tp")),
            P(("unit", "tp")),
            P(("unit", "tp")),
            P("unit"),
        ),
        check_vma=False,
    )
```

profile of v0, /device:TPU:32, one launch (start us, length us, event | category | flops | bytes accessed | tf_op | source)
XLA Modules:
  0.0 139.9 jit_solution(927208889308358699)
XLA Ops:
  7.2 0.0 copy-start
  7.2 0.0 copy-start.1
  7.2 0.0 copy-start.3
  7.2 0.0 copy-start.4
  7.2 0.0 all-gather.2.cloned.1.call-start
  7.3 0.8 copy-done
  8.0 1.4 %multiply_reduce_fusion = (f32[1024]{0:T(1024)S(1)}, f32[256,1024]{1,0:T(8,128)S(1)}) fusion(bf16[256,32]{0,1:T(8,128)(2,1)} %param.12, bf16[32,1024]{1,0:T(8,128)(2,1)S(1)} %copy-done, bf16[256,1024]{1,0:T(8,128)(2,1)} %param.11), kind=kOutput, calls=%fused_computation.7 | convolution fusion | flops 18086912 | bytes 1658880 | tf_op jit(solution)/shard_map/dot_general | solution.py:56
  9.4 1.2 multiply_reduce_fusion.1
  10.6 0.0 copy-done.1
  10.6 0.0 copy-done.3
  10.7 0.0 copy-done.4
  10.7 0.2 multiply_reduce_fusion.2
  10.9 0.1 broadcast_in_dim.4
  11.0 14.6 %all_to_all.12 = f32[16,1,1536]{2,1,0:T(1,128)S(1)} all-to-all(f32[16,1,1536]{2,1,0:T(1,128)S(1)} %broadcast_in_dim.4), channel_id=1, replica_groups=mesh['unit'=4,'zero'=16,'tp'=4] {'zero'}, dimensions={0} | all-to-all | bytes 196608 | tf_op jit(solution)/shard_map/all_to_all | solution.py:11
  25.6 0.1 reduce_sum.39
  25.7 0.0 copy-start.5
  25.7 0.0 copy-start.6
  25.8 0.0 copy-start.2
  25.8 0.0 copy-start.7
  25.8 0.0 copy-start.8
  25.8 0.1 divide_convert_fusion
  25.9 0.9 pad_maximum_fusion
  26.9 0.0 all-gather.2.cloned.1.call-update
  26.9 0.0 copy-done.5
  26.9 0.0 copy-done.6
  26.9 0.0 copy-done.2
  26.9 0.0 copy-done.7
  26.9 0.0 copy-done.8
  27.0 12.1 %all_to_all.13 = bf16[64,1,64]{2,1,0:T(2,128)(2,1)S(1)} all-to-all(bf16[64,1,64]{2,1,0:T(2,128)(2,1)S(1)} %broadcast_in_dim.10), channel_id=1, replica_groups=mesh['unit'=4,'zero'=16,'tp'=4] {'zero','tp'}, dimensions={0} | all-to-all | bytes 16384 | tf_op jit(solution)/shard_map/all_to_all | solution.py:11
  39.1 0.1 reduce.1
  39.2 0.7 reshape.29
  39.8 80.9 %all-gather.2.cloned.1.call-done = bf16[4096,1536]{1,0:T(8,128)(2,1)} async-done(((bf16[256,1536]{1,0:T(8,128)(2,1)}), bf16[4096,1536]{1,0:T(8,128)(2,1)}) %all-gather.2.cloned.1.call-update) | async-done | bytes 12582928 | tf_op jit(solution)/shard_map/all_gather | solution.py:29
  120.7 4.5 %fusion.3 = (bf16[4096,256]{1,0:T(8,128)(2,1)}, bf16[4096,256]{1,0:T(8,128)(2,1)}) fusion(bf16[4096,1536]{1,0:T(8,128)(2,1)} %all-gather.2.cloned.1.call-done), kind=kLoop, calls=%fused_computation.18 | loop fusion | bytes 8388608 | tf_op jit(solution)/shard_map/split | solution.py:30
  125.3 7.8 %split.12 = bf16[4096,1024]{1,0:T(8,128)(2,1)} slice(bf16[4096,1536]{1,0:T(8,128)(2,1)} %all-gather.2.cloned.1.call-done), slice={[0:4096], [0:1024]} | slice | bytes 16777216 | tf_op jit(solution)/shard_map/split | solution.py:30
  (6 shorter events, 0.1 us)
Async XLA Ops:
  7.2 0.8 copy-start
  7.2 3.5 %copy-start.1 = (bf16[256,256]{1,0:T(8,128)(2,1)S(1)}, bf16[256,256]{1,0:T(8,128)(2,1)}, u32[]{:S(2)}) copy-start(bf16[256,256]{1,0:T(8,128)(2,1)} %param.14) | copy-start | bytes 393220
  7.2 3.5 %copy-start.3 = (bf16[256,32]{0,1:T(8,128)(2,1)S(1)}, bf16[256,32]{0,1:T(8,128)(2,1)}, u32[]{:S(2)}) copy-start(bf16[256,32]{0,1:T(8,128)(2,1)} %param.15) | copy-start | bytes 49156
  7.2 3.5 %copy-start.4 = (bf16[32,256]{1,0:T(8,128)(2,1)S(1)}, bf16[32,256]{1,0:T(8,128)(2,1)}, u32[]{:S(2)}) copy-start(bf16[32,256]{1,0:T(8,128)(2,1)} %param.16) | copy-start | bytes 49156
  7.2 113.5 %all-gather.2.cloned.1.call-start = ((), (), s32[]{:S(2)}) async-start(), calls=%async_computation.2 | async-start | bytes 13369344 | tf_op jit(solution)/shard_map/all_gather | solution.py:29
  25.7 1.2 copy-start.5
  25.7 1.2 copy-start.6
  25.8 1.2 copy-start.2
  25.8 1.2 copy-start.7
  25.8 1.2 copy-start.8
Sparse Core Ops, SparseCore 0:
  27.0 93.6 all-gather.1
where the time goes:
time: 141 us; the launch traced here: 140 us
  waiting for transfers between devices  80.9 us (57%)
  blocking collectives  26.7 us (19%)
  between operations  14.2 us (10%)
  local copies, waits for them, and re-layouts  13.9 us (10%)
  matrix products  2.85 us (2%)
    all_gather x1, waiting for transfers between devices, side_by_side(): filled = lax.all_gather(both, axis, axis=dim, tiled=True)  80.9 us
    all_to_all x2, blocking collectives, from_everyone(): return lax.all_to_all(copies, axis, split_axis=0, concat_axis=0, tiled=True)  26.7 us
    split x2, local copies, waits for them, and re-layouts, side_by_side(): jnp.split(filled, [sum(widths[:k]) for k in range(1, len(widths))], axis=...  12.3 us
  transfers between devices with their start and end apart: 1, of which 1 were waited for; matrix products, arithmetic and copies ran while one was open for 1% of the time, Pallas kernels for 0%

commit v1 on v0

v1 whole, which is shorter than its diff:
```python
import jax
import jax.numpy as jnp
from jax import lax
from jax.experimental import pallas as pl
from jax.experimental.pallas import tpu as pltpu
from jax.sharding import PartitionSpec as P

MESH = pl.DeviceIdType.MESH
SIDE = 4
BLOCKS = SIDE * SIDE
TP = 4
RANK = 32
ROWS = 256
Q, KV = 1024, 256
COLS = Q + 2 * KV
AHEAD = 4
DIRECTIONS = ((0, 1), (0, -1), (1, 1), (1, -1))

BULK = [(0, 1, 1), (0, 1, 1), (0, 1, -1), (0, -1, 1), (0, -1, -1), (0, -1, -1)]
BULK = BULK + [(1, s1, s2) for _, s1, s2 in BULK]
BULK_PLACE = [("q", 0), ("q", 1), ("k", 0), ("q", 2), ("v", 0), ("q", 3)]
BULK_PLACE = BULK_PLACE + [("q", 4), ("q", 5), ("k", 1), ("q", 6), ("v", 1), ("q", 7)]
SMALL = [(0, 1, 1), (1, -1, -1), (1, 1, 1)]


def children(tree, a, b):
    first, far1, far2 = tree
    out = []
    for axis, sign, here, far, along in (
        (first, 1, a, far1, 0),
        (first, -1, a, far1, 0),
        (1 - first, 1, b, far2, 1),
        (1 - first, -1, b, far2, 1),
    ):
        if along == 0 and b != 0:
            continue
        goes = here == 0 or (here == sign % SIDE and far == sign)
        if goes:
            to = (here + sign) % SIDE
            out.append(((axis, sign), (to, b) if along == 0 else (a, to)))
    return out


def depth(tree, a, b):
    return max((1 + depth(tree, *to) for _, to in children(tree, a, b)), default=0)


def offsets(tree, a, b):
    return (b, a) if tree[0] == 0 else (a, b)


def plan(trees, ahead, one_per_step):
    ready = {d: [] for d in DIRECTIONS}

    def offer(c, a, b, at):
        for d, to in children(trees[c], a, b):
            ready[d].append((at, c, a, b, to))

    for c in range(len(trees)):
        offer(c, 0, 0, -ahead)
    steps = []
    while any(ready.values()):
        s = len(steps)
        now = {}
        for d in DIRECTIONS:
            can = [r for r in ready[d] if r[0] <= s - ahead]
            can.sort(key=lambda r: (-depth(trees[r[1]], *r[4]), r[0], r[1]))
            now[d] = can[:1] if one_per_step else can
            for r in now[d]:
                ready[d].remove(r)
        for d in DIRECTIONS:
            for _, c, a, b, to in now[d]:
                offer(c, *to, s)
        steps.append({d: [r[1:] for r in now[d]] for d in DIRECTIONS})
    return steps


STEPS = plan(BULK, AHEAD, True)
SMALL_STEPS = plan(SMALL, AHEAD, False)
N = len(STEPS)


def gather_kernel(
    wq, wk, wv, lq, lk, lv, hq, hk, hv, train, step_in,
    rq, rk, rv, low, sums, norms,
    load_sem, send_sem, recv_sem, small_send, small_recv, tp_send, tp_recv,
):
    me = lax.axis_index("zero")
    t = lax.axis_index("tp")
    y, x = me // SIDE, me % SIDE

    def block(dy, dx):
        return ((y + SIDE - dy) % SIDE) * SIDE + (x + SIDE - dx) % SIDE

    blk = {(dy, dx): block(dy, dx) for dy in range(SIDE) for dx in range(SIDE)}
    towards = {
        (axis, sign): blk[(0, -sign % SIDE) if axis == 0 else (-sign % SIDE, 0)]
        for axis, sign in DIRECTIONS
    }

    barrier = pltpu.get_barrier_semaphore()
    for d in DIRECTIONS:
        pl.semaphore_signal(barrier, inc=1, device_id={"zero": towards[d]}, device_id_type=MESH)
    for i in range(1, TP):
        pl.semaphore_signal(barrier, inc=1, device_id={"tp": (t + i) % TP}, device_id_type=MESH)

    loads = [
        pltpu.make_async_copy(src, dst.at[me], load_sem.at[i])
        for i, (src, dst) in enumerate(((wq, rq), (wk, rk), (wv, rv)))
    ]
    for load in loads:
        load.start()

    @pl.when(t == 0)
    def _():
        low[t, me] = lq[...]

    @pl.when(t == 1)
    def _():
        low[t, me] = lk[...]

    @pl.when(t >= 2)
    def _():
        low[t, me] = lv[...]

    for load in loads:
        load.wait()
    pl.semaphore_wait(barrier, len(DIRECTIONS) + TP - 1)

    def bulk_ref(c, a, b):
        which, i = BULK_PLACE[c]
        ref = {"q": rq, "k": rk, "v": rv}[which]
        rows = 32 if which == "q" else 128
        return ref.at[blk[offsets(BULK[c], a, b)], pl.ds(rows * i, rows)]

    def bulk_copy(s, k, opposite):
        d = DIRECTIONS[k]
        c, a, b, to = STEPS[s][d][0]
        ref = bulk_ref(c, *(to if opposite else (a, b)))
        return pltpu.make_async_remote_copy(
            src_ref=ref, dst_ref=ref, send_sem=send_sem.at[k, s], recv_sem=recv_sem.at[k, s],
            device_id={"zero": towards[d]}, device_id_type=MESH,
        )

    def small_copy(c, a, b, to, d, opposite):
        where = blk[offsets(SMALL[c], *(to if opposite else (a, b)))]
        ref = sums.at[where] if c == 2 else low.at[t, where, pl.ds(16 * c, 16)]
        slot = to[0] * SIDE + to[1]
        return pltpu.make_async_remote_copy(
            src_ref=ref, dst_ref=ref, send_sem=small_send.at[c, slot], recv_sem=small_recv.at[c, slot],
            device_id={"zero": towards[d]}, device_id_type=MESH,
        )

    def smalls(s):
        if 0 <= s < len(SMALL_STEPS):
            for d in DIRECTIONS:
                for c, a, b, to in SMALL_STEPS[s][d]:
                    yield (c, a, b, to, d)

    def sends(s):
        for k, d in enumerate(DIRECTIONS):
            if s < N and STEPS[s][d]:
                bulk_copy(s, k, False).start()

    def receives(s):
        for k, d in enumerate(DIRECTIONS):
            if 0 <= s < N and STEPS[s][d]:
                bulk_copy(s, k, True).wait_recv()

    for s in range(AHEAD):
        sends(s)

    for w, lo, hi, start in ((rq, lq, hq, 0), (rk, lk, hk, Q), (rv, lv, hv, Q + KV)):
        left = lo[...]
        for j in range(w.shape[2] // KV):
            cols = pl.ds(KV * j, KV)
            fresh = w[me, :, cols].astype(jnp.float32) + 2.0 * lax.dot_general(
                left, hi[:, cols], (((0,), (0,)), ((), ())), preferred_element_type=jnp.float32
            )
            sums[me, :, pl.ds(start + KV * j, KV)] = jnp.sum(fresh * fresh, axis=0, keepdims=True)
    sums[me, :, pl.ds(COLS, 128)] = jnp.concatenate([train[...] + step_in[...]] * 2, axis=1)

    lag = AHEAD + 1
    last_small = len(SMALL_STEPS) - 1 + lag
    for s in range(AHEAD, N + AHEAD):
        receives(s - AHEAD)
        for item in smalls(s - lag - AHEAD):
            small_copy(*item, True).wait_recv()
        sends(s)
        for item in smalls(s - lag):
            small_copy(*item, False).start()
        if s == last_small + AHEAD:
            for i in range(1, TP):
                for copy in tp_copies(low, sums, norms, t, t, i, tp_send, tp_recv):
                    copy.start()
    for i in range(1, TP):
        for copy in tp_copies(low, sums, norms, t, (t + TP - i) % TP, i, tp_send, tp_recv):
            copy.wait_recv()
    norms[t] = sums[:, 0, pl.ds(COLS, 128)]
    for i in range(1, TP):
        for copy in tp_copies(low, sums, norms, t, t, i, tp_send, tp_recv):
            copy.wait_send()
    for s in range(len(SMALL_STEPS)):
        for item in smalls(s):
            small_copy(*item, False).wait_send()
    for s in range(N):
        for k, d in enumerate(DIRECTIONS):
            if STEPS[s][d]:
                bulk_copy(s, k, False).wait_send()


def tp_copies(low, sums, norms, t, owner, i, send_sem, recv_sem):
    for j, (src, dst) in enumerate(
        ((low.at[owner], low.at[owner]), (sums.at[:, 0, pl.ds(COLS, 128)], norms.at[owner]))
    ):
        yield pltpu.make_async_remote_copy(
            src_ref=src, dst_ref=dst, send_sem=send_sem.at[i, j], recv_sem=recv_sem.at[i, j],
            device_id={"tp": (t + i) % TP}, device_id_type=MESH,
        )


SLOTS = 4


def merge_kernel(
    rq, rk, rv, low, sums, norms, hq, hk, hv,
    sq, sk, sv, cq, ck, cv, norm_out,
    inv, oq, ok, ov, lines, out_sem,
):
    total = sums[0, :, pl.ds(0, COLS)]
    for b in range(1, BLOCKS):
        total = total + sums[b, :, pl.ds(0, COLS)]
    column = jnp.sqrt(total)
    cq[...] = column[:, :Q]
    ck[...] = column[:, Q : Q + KV]
    cv[...] = column[:, Q + KV :]
    inv[...] = 1.0 / column

    lane = lax.broadcasted_iota(jnp.int32, (BLOCKS, 128), 1)
    for p in range(2):
        lines[pl.ds(p, BLOCKS, stride=2), :] = jnp.where(lane < 64, norms[2 * p], norms[2 * p + 1])
    norm_out[...] = lines[...].astype(jnp.bfloat16)

    parts = ((rq, 0, hq, oq, sq, 0), (rk, 1, hk, ok, sk, Q), (rv, 2, hv, ov, sv, Q + KV))

    def outs(b, slot):
        return [
            pltpu.make_async_copy(o.at[slot], serve.at[pl.ds(b * ROWS, ROWS)], out_sem.at[i, slot])
            for i, (_, _, _, o, serve, _) in enumerate(parts)
        ]

    def one(b, _):
        slot = b % SLOTS

        @pl.when(b >= SLOTS)
        def _():
            for copy in outs(b - SLOTS, slot):
                copy.wait()

        for w, which, hi, o, _, start in parts:
            left = low[which, b]
            for j in range(w.shape[2] // KV):
                cols = pl.ds(KV * j, KV)
                fresh = w[b, :, cols].astype(jnp.float32) + lax.dot_general(
                    left, 2.0 * hi[:, cols], (((0,), (0,)), ((), ())), preferred_element_type=jnp.float32
                )
                o[slot, :, cols] = (fresh * inv[:, pl.ds(start + KV * j, KV)]).astype(jnp.bfloat16)
        for copy in outs(b, slot):
            copy.start()
        return 0

    lax.fori_loop(0, BLOCKS, one, 0)
    for b in range(BLOCKS - SLOTS, BLOCKS):
        for copy in outs(b, b % SLOTS):
            copy.wait()


def on_device(
    weight_query, low_query, high_query,
    weight_key, low_key, high_key,
    weight_value, low_value, high_value,
    norm_train, norm_step,
):
    f32, bf16 = jnp.float32, jnp.bfloat16
    vmem = pl.BlockSpec(memory_space=pltpu.VMEM)
    hbm = pl.BlockSpec(memory_space=pl.ANY)
    highs = (high_query, high_key, high_value)
    dma = pltpu.SemaphoreType.DMA
    gathered = pl.pallas_call(
        gather_kernel,
        name="gather",
        out_shape=(
            pltpu.VMEM((BLOCKS, ROWS, Q), bf16),
            pltpu.VMEM((BLOCKS, ROWS, KV), bf16),
            pltpu.VMEM((BLOCKS, ROWS, KV), bf16),
            pltpu.VMEM((TP, BLOCKS, RANK, ROWS), bf16),
            pltpu.VMEM((BLOCKS, 1, COLS + 128), f32),
            pltpu.VMEM((TP, BLOCKS, 128), f32),
        ),
        in_specs=[hbm] * 3 + [vmem] * 8,
        out_specs=[vmem] * 6,
        scratch_shapes=[
            dma((3,)), dma((4, N)), dma((4, N)), dma((3, BLOCKS)), dma((3, BLOCKS)), dma((TP, 2)), dma((TP, 2)),
        ],
        compiler_params=pltpu.CompilerParams(collective_id=0, has_side_effects=True, vmem_limit_bytes=16 << 20),
    )(
        weight_query, weight_key, weight_value, low_query.T, low_key.T, low_value.T, *highs,
        norm_train.reshape(1, 64), norm_step.reshape(1, 64),
    )
    sq, sk, sv, cq, ck, cv, norm = pl.pallas_call(
        merge_kernel,
        name="merge",
        out_shape=(
            jax.ShapeDtypeStruct((BLOCKS * ROWS, Q), bf16),
            jax.ShapeDtypeStruct((BLOCKS * ROWS, KV), bf16),
            jax.ShapeDtypeStruct((BLOCKS * ROWS, KV), bf16),
            jax.ShapeDtypeStruct((1, Q), f32),
            jax.ShapeDtypeStruct((1, KV), f32),
            jax.ShapeDtypeStruct((1, KV), f32),
            jax.ShapeDtypeStruct((32, 128), bf16),
        ),
        in_specs=[vmem] * 9,
        out_specs=[hbm] * 3 + [vmem] * 4,
        scratch_shapes=[
            pltpu.VMEM((1, COLS), f32),
            pltpu.VMEM((SLOTS, ROWS, Q), bf16),
            pltpu.VMEM((SLOTS, ROWS, KV), bf16),
            pltpu.VMEM((SLOTS, ROWS, KV), bf16),
            pltpu.VMEM((2 * BLOCKS, 128), f32),
            dma((3, SLOTS)),
        ],
        compiler_params=pltpu.CompilerParams(vmem_limit_bytes=24 << 20),
    )(*gathered, *highs)
    return sq, sk, sv, cq.reshape(Q), ck.reshape(KV), cv.reshape(KV), norm.reshape(4096)


def solution(mesh):
    rows = P(("unit", "zero"), "tp")
    low = P(("unit", "zero"), None)
    high = P("unit", "tp")
    norm = P(("unit", "zero", "tp"))
    return jax.shard_map(
        on_device,
        mesh=mesh,
        in_specs=(rows, low, high) * 3 + (norm, norm),
        out_specs=(high, high, high, P(("unit", "tp")), P(("unit", "tp")), P(("unit", "tp")), P("unit")),
        check_vma=False,
    )
```

time: 141 us -> 96.4 us (0.68)
  Pallas kernels: 0 us -> 84.1 us
  waiting for transfers between devices: 80.9 us -> 0 us
  blocking collectives: 26.7 us -> 0 us
  between operations: 14.2 us -> 0.67 us
  local copies, waits for them, and re-layouts: 13.9 us -> 10.8 us
  matrix products: 2.85 us -> 0 us
    pallas_call x0 -> x2, Pallas kernels: none -> 84.1 us  [the longest x1 76.2 us: on_device(): pl.pallas_call(gather_kernel, name='gather', out_shape=(pltpu.VMEM((BLOCK...]
    all_gather x1 -> x0, waiting for transfers between devices: 80.9 us -> none  [side_by_side(): filled = lax.all_gather(both, axis, axis=dim, tiled=True)]
    all_to_all x2 -> x0, blocking collectives: 26.7 us -> none  [from_everyone(): return lax.all_to_all(copies, axis, split_axis=0, concat_axis=0, tiled=True)]
    split x2 -> x0, local copies, waits for them, and re-layouts: 12.3 us -> none  [side_by_side(): jnp.split(filled, [sum(widths[:k]) for k in range(1, len(widths))], axis=...]
    unnamed x18 -> x28, local copies, waits for them, and re-layouts: 0.81 us -> 10.8 us
    dot_general x3 -> x0, matrix products: 2.85 us -> none  [the longest x1 1.42 us: on_device(): jnp.dot(low_query, high_query, preferred_element_type=jnp.float32)]
  transfers between devices with their start and end apart: 1 -> 0, of which waited for: 1 -> 0; matrix products, arithmetic and copies ran while one was open for 1% -> 0% of each run, Pallas kernels for 0% -> 0%
where the time goes in v1:
time: 96.4 us; the launch traced here: 95.6 us
  Pallas kernels  84.1 us (87%)
  local copies, waits for them, and re-layouts  10.8 us (11%)
    pallas_call x1, Pallas kernels, on_device(): pl.pallas_call(gather_kernel, name='gather', out_shape=(pltpu.VMEM((BLOCK...  76.2 us
    unnamed x28, local copies, waits for them, and re-layouts  10.8 us
    pallas_call x1, Pallas kernels, on_device(): pl.pallas_call(merge_kernel, name='merge', out_shape=(jax.ShapeDtypeStruc...  7.87 us

profile of v1, /device:TPU:32, one launch (start us, length us, event | category | flops | bytes accessed | tf_op | source)
XLA Modules:
  0.0 95.6 jit_solution(3106838245150524264)
XLA Ops:
  0.6 0.0 copy-start
  0.6 1.0 %copy-done = bf16[256,1024]{1,0:T(8,128)(2,1)S(1)} copy-done((bf16[256,1024]{1,0:T(8,128)(2,1)S(1)}, bf16[256,1024]{1,0:T(8,128)(2,1)}, u32[]{:S(2)}) %copy-start) | copy-done | bytes 524312
  1.7 0.0 copy-start.1
  1.7 0.8 copy-done.1
  2.5 0.0 copy-start.3
  2.5 0.9 copy-done.3
  3.4 0.0 copy-start.4
  3.4 0.9 copy-done.4
  4.3 0.0 copy-start.5
  4.3 0.7 copy-done.5
  5.0 0.0 copy-start.7
  5.0 0.7 copy-done.7
  5.8 0.0 copy-start.9
  5.8 0.7 copy-done.9
  6.5 0.0 copy-start.10
  6.5 0.7 copy-done.10
  7.2 0.0 copy-start.11
  7.2 0.7 copy-done.11
  7.9 0.0 copy-start.12
  7.9 0.7 copy-done.12
  8.6 0.0 copy-start.13
  8.6 0.7 copy-done.13
  9.2 76.2 %gather.1 = (bf16[16,256,1024]{2,1,0:T(8,128)(2,1)S(1)}, bf16[16,256,256]{2,1,0:T(8,128)(2,1)S(1)}, bf16[16,256,256]{2,1,0:T(8,128)(2,1)S(1)}, bf16[4,16,32,256]...) custom-call(bf16[256,1024]{1,0:T(8,128)(2,1)S(1)} %copy-done, ...), custom_call_target="tpu_custom_call" | custom-call | tf_op jit(solution)/shard_map/gather/pallas_call | solution.py:289
  85.4 0.0 copy-start.2
  85.5 0.8 copy-done.2
  86.3 0.0 copy-start.6
  86.3 0.7 copy-done.6
  87.0 0.0 copy-start.8
  87.0 0.7 copy-done.8
  87.7 7.9 %merge.1 = (bf16[4096,1024]{1,0:T(8,128)(2,1)}, bf16[4096,256]{1,0:T(8,128)(2,1)}, bf16[4096,256]{1,0:T(8,128)(2,1)}, f32[1,1024]{1,0:T(1,128)}, f32[1,256]{1,0:...) custom-call(bf16[16,256,1024]{2,1,0:T(8,128)(2,1)S(1)} %get-tuple-element.20.rq, ...), custom_call_target="tpu_custom_call" | custom-call | tf_op jit(solution)/shard_map/merge/pallas_call | solution.py:310
Async XLA Ops:
  0.6 1.0 %copy-start = (bf16[256,1024]{1,0:T(8,128)(2,1)S(1)}, bf16[256,1024]{1,0:T(8,128)(2,1)}, u32[]{:S(2)}) copy-start(bf16[256,1024]{1,0:T(8,128)(2,1)} %wq.1) | copy-start | bytes 1572868
  1.7 0.8 copy-start.1
  2.5 0.9 copy-start.3
  3.4 0.9 copy-start.4
  4.3 0.7 copy-start.5
  5.0 0.7 copy-start.7
  5.8 0.7 copy-start.9
  6.5 0.7 copy-start.10
  7.2 0.7 copy-start.11
  7.9 0.7 copy-start.12
  8.6 0.7 copy-start.13
  85.4 0.8 copy-start.2
  86.3 0.7 copy-start.6
  87.0 0.7 copy-start.8

commit v2 on v1

v2 whole, which is shorter than its diff:
```python
import jax
import jax.numpy as jnp
from jax import lax
from jax.experimental import pallas as pl
from jax.experimental.pallas import tpu as pltpu
from jax.sharding import PartitionSpec as P

MESH = pl.DeviceIdType.MESH
SIDE = 4
BLOCKS = SIDE * SIDE
TP = 4
RANK = 32
ROWS = 256
Q, KV = 1024, 256
COLS = Q + 2 * KV
AHEAD = 4
TP_WAIT = 10
DIRECTIONS = ((0, 1), (0, -1), (1, 1), (1, -1))

BULK = [(0, 1, 1), (0, 1, 1), (0, 1, -1), (0, -1, 1), (0, -1, -1), (0, -1, -1)]
BULK = BULK + [(1, s1, s2) for _, s1, s2 in BULK]
BULK_PLACE = [("q", 0), ("q", 1), ("k", 0), ("q", 2), ("v", 0), ("q", 3)]
BULK_PLACE = BULK_PLACE + [("q", 4), ("q", 5), ("k", 1), ("q", 6), ("v", 1), ("q", 7)]
SMALL = [(0, 1, 1), (1, -1, -1), (1, 1, 1)]


def children(tree, a, b):
    first, far1, far2 = tree
    out = []
    for axis, sign, here, far, along in (
        (first, 1, a, far1, 0),
        (first, -1, a, far1, 0),
        (1 - first, 1, b, far2, 1),
        (1 - first, -1, b, far2, 1),
    ):
        if along == 0 and b != 0:
            continue
        goes = here == 0 or (here == sign % SIDE and far == sign)
        if goes:
            to = (here + sign) % SIDE
            out.append(((axis, sign), (to, b) if along == 0 else (a, to)))
    return out


def depth(tree, a, b):
    return max((1 + depth(tree, *to) for _, to in children(tree, a, b)), default=0)


def offsets(tree, a, b):
    return (b, a) if tree[0] == 0 else (a, b)


def plan(trees, ahead, one_per_step):
    ready = {d: [] for d in DIRECTIONS}

    def offer(c, a, b, at):
        for d, to in children(trees[c], a, b):
            ready[d].append((at, c, a, b, to))

    for c in range(len(trees)):
        offer(c, 0, 0, -ahead)
    steps = []
    while any(ready.values()):
        s = len(steps)
        now = {}
        for d in DIRECTIONS:
            can = [r for r in ready[d] if r[0] <= s - ahead]
            can.sort(key=lambda r: (-depth(trees[r[1]], *r[4]), r[0], r[1]))
            now[d] = can[:1] if one_per_step else can
            for r in now[d]:
                ready[d].remove(r)
        for d in DIRECTIONS:
            for _, c, a, b, to in now[d]:
                offer(c, *to, s)
        steps.append({d: [r[1:] for r in now[d]] for d in DIRECTIONS})
    return steps


STEPS = plan(BULK, AHEAD, True)
SMALL_STEPS = plan(SMALL, AHEAD, False)
N = len(STEPS)


def gather_kernel(
    wq, wk, wv, lq, lk, lv, hq, hk, hv, train, step_in,
    rq, rk, rv, left, high2, inv, column, norm_out,
    own_low, high, norm_in, low, sums, norms, lines,
    load_sem, send_sem, recv_sem, small_send, small_recv, tp_send, tp_recv,
):
    me = lax.axis_index("zero")
    t = lax.axis_index("tp")
    y, x = me // SIDE, me % SIDE

    def block(dy, dx):
        return ((y + SIDE - dy) % SIDE) * SIDE + (x + SIDE - dx) % SIDE

    blk = {(dy, dx): block(dy, dx) for dy in range(SIDE) for dx in range(SIDE)}
    towards = {
        (axis, sign): blk[(0, -sign % SIDE) if axis == 0 else (-sign % SIDE, 0)]
        for axis, sign in DIRECTIONS
    }

    barrier = pltpu.get_barrier_semaphore()
    for d in DIRECTIONS:
        pl.semaphore_signal(barrier, inc=1, device_id={"zero": towards[d]}, device_id_type=MESH)
    for i in range(1, TP):
        pl.semaphore_signal(barrier, inc=1, device_id={"tp": (t + i) % TP}, device_id_type=MESH)

    loads = [
        pltpu.make_async_copy(src, dst, load_sem.at[i])
        for i, (src, dst) in enumerate(
            (
                (wq, rq.at[me]), (wk, rk.at[me]), (wv, rv.at[me]),
                (lq, own_low.at[0]), (lk, own_low.at[1]), (lv, own_low.at[2]),
                (hq, high.at[:, pl.ds(0, Q)]), (hk, high.at[:, pl.ds(Q, KV)]), (hv, high.at[:, pl.ds(Q + KV, KV)]),
                (train, norm_in.at[0]), (step_in, norm_in.at[1]),
            )
        )
    ]
    for load in loads:
        load.start()
    for load in loads[:3]:
        load.wait()
    pl.semaphore_wait(barrier, len(DIRECTIONS) + TP - 1)

    def bulk_ref(c, a, b):
        which, i = BULK_PLACE[c]
        ref = {"q": rq, "k": rk, "v": rv}[which]
        rows = 32 if which == "q" else 128
        return ref.at[blk[offsets(BULK[c], a, b)], pl.ds(rows * i, rows)]

    def bulk_copy(s, k, opposite):
        d = DIRECTIONS[k]
        c, a, b, to = STEPS[s][d][0]
        ref = bulk_ref(c, *(to if opposite else (a, b)))
        return pltpu.make_async_remote_copy(
            src_ref=ref, dst_ref=ref, send_sem=send_sem.at[k, s], recv_sem=recv_sem.at[k, s],
            device_id={"zero": towards[d]}, device_id_type=MESH,
        )

    def small_copy(c, a, b, to, d, opposite):
        where = blk[offsets(SMALL[c], *(to if opposite else (a, b)))]
        ref = sums.at[where] if c == 2 else low.at[t, where, pl.ds(16 * c, 16)]
        slot = to[0] * SIDE + to[1]
        return pltpu.make_async_remote_copy(
            src_ref=ref, dst_ref=ref, send_sem=small_send.at[c, slot], recv_sem=small_recv.at[c, slot],
            device_id={"zero": towards[d]}, device_id_type=MESH,
        )

    def smalls(s):
        if 0 <= s < len(SMALL_STEPS):
            for d in DIRECTIONS:
                for c, a, b, to in SMALL_STEPS[s][d]:
                    yield (c, a, b, to, d)

    def tp_copies(owner, i):
        for j, (src, dst) in enumerate(
            ((low.at[owner], low.at[owner]), (sums.at[:, 0, pl.ds(COLS, 128)], norms.at[owner]))
        ):
            yield pltpu.make_async_remote_copy(
                src_ref=src, dst_ref=dst, send_sem=tp_send.at[i, j], recv_sem=tp_recv.at[i, j],
                device_id={"tp": (t + i) % TP}, device_id_type=MESH,
            )

    def sends(s):
        for k, d in enumerate(DIRECTIONS):
            if s < N and STEPS[s][d]:
                bulk_copy(s, k, False).start()

    def receives(s):
        for k, d in enumerate(DIRECTIONS):
            if 0 <= s < N and STEPS[s][d]:
                bulk_copy(s, k, True).wait_recv()

    for s in range(AHEAD):
        sends(s)
    for load in loads[3:]:
        load.wait()

    @pl.when(t == 0)
    def _():
        low[t, me] = own_low[0]

    @pl.when(t == 1)
    def _():
        low[t, me] = own_low[1]

    @pl.when(t >= 2)
    def _():
        low[t, me] = own_low[2]

    high2[...] = high[...] * 2.0

    for which, w, start in ((0, rq, 0), (1, rk, Q), (2, rv, Q + KV)):
        rows = own_low[which]
        for j in range(w.shape[2] // KV):
            cols = pl.ds(start + KV * j, KV)
            fresh = w[me, :, pl.ds(KV * j, KV)].astype(jnp.float32) + lax.dot_general(
                rows, high2[:, cols], (((0,), (0,)), ((), ())), preferred_element_type=jnp.float32
            )
            sums[me, :, cols] = jnp.sum(fresh * fresh, axis=0, keepdims=True)
    sums[me, :, pl.ds(COLS, 128)] = jnp.concatenate([norm_in[0] + norm_in[1]] * 2, axis=1)

    def scales():
        total = sums[0, :, pl.ds(0, COLS)]
        for b in range(1, BLOCKS):
            total = total + sums[b, :, pl.ds(0, COLS)]
        scale = jnp.sqrt(total)
        column[...] = scale
        inv[...] = 1.0 / scale
        norms[t] = sums[:, 0, pl.ds(COLS, 128)]
        lane = lax.broadcasted_iota(jnp.int32, (BLOCKS, 128), 1)
        for p in range(2):
            lines[pl.ds(p, BLOCKS, stride=2), :] = jnp.where(lane < 64, norms[2 * p], norms[2 * p + 1])
        norm_out[...] = lines[...].astype(jnp.bfloat16)

    lag = AHEAD + 1
    last_small = len(SMALL_STEPS) - 1 + lag + AHEAD
    done = 0
    for s in range(AHEAD, N + AHEAD):
        receives(s - AHEAD)
        for item in smalls(s - lag - AHEAD):
            small_copy(*item, True).wait_recv()
        sends(s)
        for item in smalls(s - lag):
            small_copy(*item, False).start()
        if s == last_small:
            for i in range(1, TP):
                for copy in tp_copies(t, i):
                    copy.start()
        if s == last_small + TP_WAIT:
            for i in range(1, TP):
                for copy in tp_copies((t + TP - i) % TP, i):
                    copy.wait_recv()
            scales()
        if s > last_small + TP_WAIT:
            while done < BLOCKS and done < 2 * (s - last_small - TP_WAIT):
                for which in range(3):
                    left[which, done] = low[which, done].T
                done += 1
    assert done == BLOCKS
    for i in range(1, TP):
        for copy in tp_copies(t, i):
            copy.wait_send()
    for s in range(len(SMALL_STEPS)):
        for item in smalls(s):
            small_copy(*item, False).wait_send()
    for s in range(N):
        for k, d in enumerate(DIRECTIONS):
            if STEPS[s][d]:
                bulk_copy(s, k, False).wait_send()


def merge_kernel(
    rq, rk, rv, left, high2, inv, column, norm,
    sq, sk, sv, cq, ck, cv, norm_out,
    oq, ok, ov, out_sem, end_sem,
):
    ends = [
        pltpu.make_async_copy(src, dst, end_sem.at[i])
        for i, (src, dst) in enumerate(
            (
                (column.at[:, pl.ds(0, Q)], cq),
                (column.at[:, pl.ds(Q, KV)], ck),
                (column.at[:, pl.ds(Q + KV, KV)], cv),
                (norm, norm_out),
            )
        )
    ]
    for copy in ends:
        copy.start()

    parts = ((rq, 0, oq, sq, 0), (rk, 1, ok, sk, Q), (rv, 2, ov, sv, Q + KV))

    def outs(b):
        return [
            pltpu.make_async_copy(o.at[b], serve.at[pl.ds(b * ROWS, ROWS)], out_sem.at[i, b])
            for i, (_, _, o, serve, _) in enumerate(parts)
        ]

    def one(b, _):
        for w, which, o, _, start in parts:
            rows = left[which, b]
            for j in range(w.shape[2] // KV):
                cols = pl.ds(KV * j, KV)
                every = pl.ds(start + KV * j, KV)
                fresh = w[b, :, cols].astype(jnp.float32) + jnp.dot(
                    rows, high2[:, every], preferred_element_type=jnp.float32
                )
                o[b, :, cols] = (fresh * inv[:, every]).astype(jnp.bfloat16)
        for copy in outs(b):
            copy.start()
        return 0

    lax.fori_loop(0, BLOCKS, one, 0)

    def end(b, _):
        for copy in outs(b):
            copy.wait()
        return 0

    lax.fori_loop(0, BLOCKS, end, 0)
    for copy in ends:
        copy.wait()


def on_device(
    weight_query, low_query, high_query,
    weight_key, low_key, high_key,
    weight_value, low_value, high_value,
    norm_train, norm_step,
):
    f32, bf16 = jnp.float32, jnp.bfloat16
    vmem = pl.BlockSpec(memory_space=pltpu.VMEM)
    hbm = pl.BlockSpec(memory_space=pltpu.HBM)
    dma = pltpu.SemaphoreType.DMA
    inputs = (
        weight_query, weight_key, weight_value, low_query.T, low_key.T, low_value.T, high_query, high_key, high_value,
        norm_train.reshape(1, 64), norm_step.reshape(1, 64),
    )
    gathered = pl.pallas_call(
        gather_kernel,
        name="gather",
        out_shape=(
            pltpu.VMEM((BLOCKS, ROWS, Q), bf16),
            pltpu.VMEM((BLOCKS, ROWS, KV), bf16),
            pltpu.VMEM((BLOCKS, ROWS, KV), bf16),
            pltpu.VMEM((3, BLOCKS, ROWS, RANK), bf16),
            pltpu.VMEM((RANK, COLS), bf16),
            pltpu.VMEM((1, COLS), f32),
            pltpu.VMEM((1, COLS), f32),
            pltpu.VMEM((2 * BLOCKS, 128), bf16),
        ),
        in_specs=[hbm] * 11,
        out_specs=[vmem] * 8,
        scratch_shapes=[
            pltpu.VMEM((3, RANK, ROWS), bf16),
            pltpu.VMEM((RANK, COLS), bf16),
            pltpu.VMEM((2, 1, 64), f32),
            pltpu.VMEM((TP, BLOCKS, RANK, ROWS), bf16),
            pltpu.VMEM((BLOCKS, 1, COLS + 128), f32),
            pltpu.VMEM((TP, BLOCKS, 128), f32),
            pltpu.VMEM((2 * BLOCKS, 128), f32),
            dma((11,)), dma((4, N)), dma((4, N)), dma((3, BLOCKS)), dma((3, BLOCKS)), dma((TP, 2)), dma((TP, 2)),
        ],
        compiler_params=pltpu.CompilerParams(collective_id=0, has_side_effects=True, vmem_limit_bytes=16 << 20),
    )(*(pltpu.with_memory_space_constraint(a, pltpu.HBM) for a in inputs))
    sq, sk, sv, cq, ck, cv, norm = pl.pallas_call(
        merge_kernel,
        name="merge",
        out_shape=(
            pltpu.HBM((BLOCKS * ROWS, Q), bf16),
            pltpu.HBM((BLOCKS * ROWS, KV), bf16),
            pltpu.HBM((BLOCKS * ROWS, KV), bf16),
            pltpu.HBM((1, Q), f32),
            pltpu.HBM((1, KV), f32),
            pltpu.HBM((1, KV), f32),
            pltpu.HBM((2 * BLOCKS, 128), bf16),
        ),
        in_specs=[vmem] * 8,
        out_specs=[hbm] * 7,
        scratch_shapes=[
            pltpu.VMEM((BLOCKS, ROWS, Q), bf16),
            pltpu.VMEM((BLOCKS, ROWS, KV), bf16),
            pltpu.VMEM((BLOCKS, ROWS, KV), bf16),
            dma((3, BLOCKS)),
            dma((4,)),
        ],
        compiler_params=pltpu.CompilerParams(vmem_limit_bytes=24 << 20),
    )(*gathered)
    return sq, sk, sv, cq.reshape(Q), ck.reshape(KV), cv.reshape(KV), norm.reshape(BLOCKS * ROWS)


def solution(mesh):
    rows = P(("unit", "zero"), "tp")
    low = P(("unit", "zero"), None)
    high = P("unit", "tp")
    norm = P(("unit", "zero", "tp"))
    return jax.shard_map(
        on_device,
        mesh=mesh,
        in_specs=(rows, low, high) * 3 + (norm, norm),
        out_specs=(high, high, high, P(("unit", "tp")), P(("unit", "tp")), P(("unit", "tp")), P("unit")),
        check_vma=False,
    )
```

time: 96.4 us -> 84 us (0.87)
  local copies, waits for them, and re-layouts: 10.8 us -> 0 us
  Pallas kernels: 84.1 us -> 83.1 us
    unnamed x28 -> x0, local copies, waits for them, and re-layouts: 10.8 us -> none
    pallas_call x1, Pallas kernels: 7.87 us -> 6.67 us  [on_device(): pl.pallas_call(merge_kernel, name='merge', out_shape=(pltpu.HBM((BLOCKS *...]
where the time goes in v2:
time: 84 us; the launch traced here: 83.8 us
  Pallas kernels  83.1 us (99%)
    pallas_call x1, Pallas kernels, on_device(): pl.pallas_call(gather_kernel, name='gather', out_shape=(pltpu.VMEM((BLOCK...  76.5 us
    pallas_call x1, Pallas kernels, on_device(): pl.pallas_call(merge_kernel, name='merge', out_shape=(pltpu.HBM((BLOCKS *...  6.67 us

profile of v2, /device:TPU:32, one launch (start us, length us, event | category | flops | bytes accessed | tf_op | source)
XLA Modules:
  0.0 83.8 jit_solution(17831495725784332164)
XLA Ops:
  0.6 76.5 %gather.1 = (bf16[16,256,1024]{2,1,0:T(8,128)(2,1)S(1)}, bf16[16,256,256]{2,1,0:T(8,128)(2,1)S(1)}, bf16[16,256,256]{2,1,0:T(8,128)(2,1)S(1)}, bf16[3,16,256,32]...) custom-call(bf16[256,1024]{1,0:T(8,128)(2,1)} %wq.1, ...), custom_call_target="tpu_custom_call" | custom-call | tf_op jit(solution)/shard_map/gather/pallas_call | solution.py:321
  77.1 6.7 %merge.1 = (bf16[4096,1024]{1,0:T(8,128)(2,1)}, bf16[4096,256]{1,0:T(8,128)(2,1)}, bf16[4096,256]{1,0:T(8,128)(2,1)}, f32[1,1024]{1,0:T(1,128)}, f32[1,256]{1,0:...) custom-call(bf16[16,256,1024]{2,1,0:T(8,128)(2,1)S(1)} %get-tuple-element.22.rq, ...), custom_call_target="tpu_custom_call" | custom-call | tf_op jit(solution)/shard_map/merge/pallas_call | solution.py:348

commit v3 on v2

--- a/solution.py
+++ b/solution.py
@@ -14,6 +14,9 @@
 Q, KV = 1024, 256
 COLS = Q + 2 * KV
 AHEAD = 4
+SMALL_AT = AHEAD
+SMALL_LAG = AHEAD
+TP_AT = SMALL_AT + 4 * SMALL_LAG
 TP_WAIT = 10
 DIRECTIONS = ((0, 1), (0, -1), (1, 1), (1, -1))
 
@@ -21,7 +24,8 @@
 BULK = BULK + [(1, s1, s2) for _, s1, s2 in BULK]
 BULK_PLACE = [("q", 0), ("q", 1), ("k", 0), ("q", 2), ("v", 0), ("q", 3)]
 BULK_PLACE = BULK_PLACE + [("q", 4), ("q", 5), ("k", 1), ("q", 6), ("v", 1), ("q", 7)]
-SMALL = [(0, 1, 1), (1, -1, -1), (1, 1, 1)]
+SMALL = [0, 1, 0, 1]
+CUT = 768
 
 
 def children(tree, a, b):
@@ -50,7 +54,7 @@
     return (b, a) if tree[0] == 0 else (a, b)
 
 
-def plan(trees, ahead, one_per_step):
+def plan(trees, ahead):
     ready = {d: [] for d in DIRECTIONS}
 
     def offer(c, a, b, at):
@@ -66,7 +70,7 @@
         for d in DIRECTIONS:
             can = [r for r in ready[d] if r[0] <= s - ahead]
             can.sort(key=lambda r: (-depth(trees[r[1]], *r[4]), r[0], r[1]))
-            now[d] = can[:1] if one_per_step else can
+            now[d] = can[:1]
             for r in now[d]:
                 ready[d].remove(r)
         for d in DIRECTIONS:
@@ -76,8 +80,7 @@
     return steps
 
 
-STEPS = plan(BULK, AHEAD, True)
-SMALL_STEPS = plan(SMALL, AHEAD, False)
+STEPS = plan(BULK, AHEAD)
 N = len(STEPS)
 
 
@@ -134,37 +137,54 @@
         c, a, b, to = STEPS[s][d][0]
         ref = bulk_ref(c, *(to if opposite else (a, b)))
         return pltpu.make_async_remote_copy(
-            src_ref=ref, dst_ref=ref, send_sem=send_sem.at[k, s], recv_sem=recv_sem.at[k, s],
+            src_ref=ref, dst_ref=ref, send_sem=send_sem.at[k, s % AHEAD], recv_sem=recv_sem.at[k, s % (2 * AHEAD)],
             device_id={"zero": towards[d]}, device_id_type=MESH,
         )
 
-    def small_copy(c, a, b, to, d, opposite):
-        where = blk[offsets(SMALL[c], *(to if opposite else (a, b)))]
-        ref = sums.at[where] if c == 2 else low.at[t, where, pl.ds(16 * c, 16)]
-        slot = to[0] * SIDE + to[1]
-        return pltpu.make_async_remote_copy(
-            src_ref=ref, dst_ref=ref, send_sem=small_send.at[c, slot], recv_sem=small_recv.at[c, slot],
-            device_id={"zero": towards[d]}, device_id_type=MESH,
-        )
-
-    def smalls(s):
-        if 0 <= s < len(SMALL_STEPS):
-            for d in DIRECTIONS:
-                for c, a, b, to in SMALL_STEPS[s][d]:
-                    yield (c, a, b, to, d)
+    def small_ref(c, where):
+        if c < 2:
+            return low.at[(t, *where, pl.ds(16 * c, 16))]
+        return sums.at[(*where, slice(None), pl.ds(0, CUT) if c == 2 else pl.ds(CUT, COLS + 128 - CUT))]
+
+    def small_copies(stage, received=False):
+        for c, first in enumerate(SMALL):
+            axis = first if stage < 2 else 1 - first
+            for n, sign in enumerate((1, -1)):
+                if stage == 1 and (n == 0) != (c % 2 == 0):
+                    continue
+                behind = 0 if stage % 2 == 0 else 1
+
+                def piece(back):
+                    at = (x, y)[axis]
+                    at = (at + 2 * SIDE - sign * back) % SIDE
+                    if stage < 2:
+                        return (y, at) if axis == 0 else (at, x)
+                    line = slice(None)
+                    if stage == 3:
+                        line = pl.ds(2 * n, 2)
+                    return (line, at) if axis == 0 else (at, line)
+
+                slot = (0, 2, 3, 5)[stage] + (0 if stage == 1 else n)
+                ref = small_ref(c, piece(behind + received))
+                yield pltpu.make_async_remote_copy(
+                    src_ref=ref, dst_ref=ref, send_sem=small_send.at[c, slot], recv_sem=small_recv.at[c, slot],
+                    device_id={"zero": towards[axis, sign]}, device_id_type=MESH,
+                )
 
     def tp_copies(owner, i):
         for j, (src, dst) in enumerate(
-            ((low.at[owner], low.at[owner]), (sums.at[:, 0, pl.ds(COLS, 128)], norms.at[owner]))
+            ((low.at[owner], low.at[owner]), (sums.at[:, :, 0, pl.ds(COLS, 128)], norms.at[owner]))
         ):
             yield pltpu.make_async_remote_copy(
-                src_ref=src, dst_ref=dst, send_sem=tp_send.at[i, j], recv_sem=tp_recv.at[i, j],
+                src_ref=src, dst_ref=dst, send_sem=tp_send.at[i - 1, j], recv_sem=tp_recv.at[i - 1, j],
                 device_id={"tp": (t + i) % TP}, device_id_type=MESH,
             )
 
     def sends(s):
         for k, d in enumerate(DIRECTIONS):
             if s < N and STEPS[s][d]:
+                if s >= AHEAD:
+                    bulk_copy(s - AHEAD, k, False).wait_send()
                 bulk_copy(s, k, False).start()
 
     def receives(s):
@@ -179,15 +199,15 @@
 
     @pl.when(t == 0)
     def _():
-        low[t, me] = own_low[0]
+        low[t, y, x] = own_low[0]
 
     @pl.when(t == 1)
     def _():
-        low[t, me] = own_low[1]
+        low[t, y, x] = own_low[1]
 
     @pl.when(t >= 2)
     def _():
-        low[t, me] = own_low[2]
+        low[t, y, x] = own_low[2]
 
     high2[...] = high[...] * 2.0
 
@@ -198,54 +218,58 @@
             fresh = w[me, :, pl.ds(KV * j, KV)].astype(jnp.float32) + lax.dot_general(
                 rows, high2[:, cols], (((0,), (0,)), ((), ())), preferred_element_type=jnp.float32
             )
-            sums[me, :, cols] = jnp.sum(fresh * fresh, axis=0, keepdims=True)
-    sums[me, :, pl.ds(COLS, 128)] = jnp.concatenate([norm_in[0] + norm_in[1]] * 2, axis=1)
+            sums[y, x, :, cols] = jnp.sum(fresh * fresh, axis=0, keepdims=True)
+    sums[y, x, :, pl.ds(COLS, 128)] = jnp.concatenate([norm_in[0] + norm_in[1]] * 2, axis=1)
 
     def scales():
-        total = sums[0, :, pl.ds(0, COLS)]
+        total = sums[0, 0, :, pl.ds(0, COLS)]
         for b in range(1, BLOCKS):
-            total = total + sums[b, :, pl.ds(0, COLS)]
+            total = total + sums[b // SIDE, b % SIDE, :, pl.ds(0, COLS)]
         scale = jnp.sqrt(total)
         column[...] = scale
         inv[...] = 1.0 / scale
-        norms[t] = sums[:, 0, pl.ds(COLS, 128)]
+        norms[t] = sums[:, :, 0, pl.ds(COLS, 128)]
         lane = lax.broadcasted_iota(jnp.int32, (BLOCKS, 128), 1)
         for p in range(2):
-            lines[pl.ds(p, BLOCKS, stride=2), :] = jnp.where(lane < 64, norms[2 * p], norms[2 * p + 1])
+            lines[pl.ds(p, BLOCKS, stride=2), :] = jnp.where(
+                lane < 64, norms[2 * p].reshape(BLOCKS, 128), norms[2 * p + 1].reshape(BLOCKS, 128)
+            )
         norm_out[...] = lines[...].astype(jnp.bfloat16)
 
-    lag = AHEAD + 1
-    last_small = len(SMALL_STEPS) - 1 + lag + AHEAD
     done = 0
     for s in range(AHEAD, N + AHEAD):
         receives(s - AHEAD)
-        for item in smalls(s - lag - AHEAD):
-            small_copy(*item, True).wait_recv()
+        for stage in range(4):
+            if s == SMALL_AT + (stage + 1) * SMALL_LAG:
+                for copy in small_copies(stage, True):
+                    copy.wait_recv()
+        for stage in range(4):
+            if s == SMALL_AT + stage * SMALL_LAG:
+                for copy in small_copies(stage):
+                    copy.start()
         sends(s)
-        for item in smalls(s - lag):
-            small_copy(*item, False).start()
-        if s == last_small:
+        if s == TP_AT:
             for i in range(1, TP):
                 for copy in tp_copies(t, i):
                     copy.start()
-        if s == last_small + TP_WAIT:
+        if s == TP_AT + TP_WAIT:
             for i in range(1, TP):
                 for copy in tp_copies((t + TP - i) % TP, i):
                     copy.wait_recv()
             scales()
-        if s > last_small + TP_WAIT:
-            while done < BLOCKS and done < 2 * (s - last_small - TP_WAIT):
+        if s > TP_AT + TP_WAIT:
+            while done < min(BLOCKS, 3 * (s - TP_AT - TP_WAIT)):
                 for which in range(3):
-                    left[which, done] = low[which, done].T
+                    left[which, done] = low[which, done // SIDE, done % SIDE].T
                 done += 1
     assert done == BLOCKS
     for i in range(1, TP):
         for copy in tp_copies(t, i):
             copy.wait_send()
-    for s in range(len(SMALL_STEPS)):
-        for item in smalls(s):
-            small_copy(*item, False).wait_send()
-    for s in range(N):
+    for stage in range(4):
+        for copy in small_copies(stage):
+            copy.wait_send()
+    for s in range(N - AHEAD, N):
         for k, d in enumerate(DIRECTIONS):
             if STEPS[s][d]:
                 bulk_copy(s, k, False).wait_send()
@@ -272,14 +296,9 @@
 
     parts = ((rq, 0, oq, sq, 0), (rk, 1, ok, sk, Q), (rv, 2, ov, sv, Q + KV))
 
-    def outs(b):
-        return [
-            pltpu.make_async_copy(o.at[b], serve.at[pl.ds(b * ROWS, ROWS)], out_sem.at[i, b])
-            for i, (_, _, o, serve, _) in enumerate(parts)
-        ]
-
     def one(b, _):
-        for w, which, o, _, start in parts:
+        place = pl.ds(pl.multiple_of(b * ROWS, ROWS), ROWS)
+        for i, (w, which, o, serve, start) in enumerate(parts):
             rows = left[which, b]
             for j in range(w.shape[2] // KV):
                 cols = pl.ds(KV * j, KV)
@@ -287,19 +306,13 @@
                 fresh = w[b, :, cols].astype(jnp.float32) + jnp.dot(
                     rows, high2[:, every], preferred_element_type=jnp.float32
                 )
-                o[b, :, cols] = (fresh * inv[:, every]).astype(jnp.bfloat16)
-        for copy in outs(b):
-            copy.start()
+                o[place, cols] = (fresh * inv[:, every]).astype(jnp.bfloat16)
+            pltpu.make_async_copy(o.at[place], serve.at[place], out_sem.at[i]).start()
         return 0
 
     lax.fori_loop(0, BLOCKS, one, 0)
-
-    def end(b, _):
-        for copy in outs(b):
-            copy.wait()
-        return 0
-
-    lax.fori_loop(0, BLOCKS, end, 0)
+    for i, (_, _, o, serve, _) in enumerate(parts):
+        pltpu.make_async_copy(o, serve, out_sem.at[i]).wait()
     for copy in ends:
         copy.wait()
 
@@ -337,11 +350,11 @@
             pltpu.VMEM((3, RANK, ROWS), bf16),
             pltpu.VMEM((RANK, COLS), bf16),
             pltpu.VMEM((2, 1, 64), f32),
-            pltpu.VMEM((TP, BLOCKS, RANK, ROWS), bf16),
-            pltpu.VMEM((BLOCKS, 1, COLS + 128), f32),
-            pltpu.VMEM((TP, BLOCKS, 128), f32),
+            pltpu.VMEM((TP, SIDE, SIDE, RANK, ROWS), bf16),
+            pltpu.VMEM((SIDE, SIDE, 1, COLS + 128), f32),
+            pltpu.VMEM((TP, SIDE, SIDE, 128), f32),
             pltpu.VMEM((2 * BLOCKS, 128), f32),
-            dma((11,)), dma((4, N)), dma((4, N)), dma((3, BLOCKS)), dma((3, BLOCKS)), dma((TP, 2)), dma((TP, 2)),
+            dma((11,)), dma((4, AHEAD)), dma((4, 2 * AHEAD)), dma((4, 7)), dma((4, 7)), dma((TP - 1, 2)), dma((TP - 1, 2)),
         ],
         compiler_params=pltpu.CompilerParams(collective_id=0, has_side_effects=True, vmem_limit_bytes=16 << 20),
     )(*(pltpu.with_memory_space_constraint(a, pltpu.HBM) for a in inputs))
@@ -360,10 +373,10 @@
         in_specs=[vmem] * 8,
         out_specs=[hbm] * 7,
         scratch_shapes=[
-            pltpu.VMEM((BLOCKS, ROWS, Q), bf16),
-            pltpu.VMEM((BLOCKS, ROWS, KV), bf16),
-            pltpu.VMEM((BLOCKS, ROWS, KV), bf16),
-            dma((3, BLOCKS)),
+            pltpu.VMEM((BLOCKS * ROWS, Q), bf16),
+            pltpu.VMEM((BLOCKS * ROWS, KV), bf16),
+            pltpu.VMEM((BLOCKS * ROWS, KV), bf16),
+            dma((3,)),
             dma((4,)),
         ],
         compiler_params=pltpu.CompilerParams(vmem_limit_bytes=24 << 20),

time: 84 us -> 79.9 us (0.951)
  Pallas kernels: 83.1 us -> 79.1 us
    pallas_call x1, Pallas kernels: 76.5 us -> 72.8 us  [on_device(): pl.pallas_call(gather_kernel, name='gather', out_shape=(pltpu.VMEM((BLOCK...]
where the time goes in v3:
time: 79.9 us; the launch traced here: 79.7 us
  Pallas kernels  79.1 us (99%)
    pallas_call x1, Pallas kernels, on_device(): pl.pallas_call(gather_kernel, name='gather', out_shape=(pltpu.VMEM((BLOCK...  72.8 us
    pallas_call x1, Pallas kernels, on_device(): pl.pallas_call(merge_kernel, name='merge', out_shape=(pltpu.HBM((BLOCKS *...  6.25 us

profile of v3, /device:TPU:32, one launch (start us, length us, event | category | flops | bytes accessed | tf_op | source)
XLA Modules:
  0.0 79.7 jit_solution(16842799481777455663)
XLA Ops:
  0.6 72.8 %gather.1 = (bf16[16,256,1024]{2,1,0:T(8,128)(2,1)S(1)}, bf16[16,256,256]{2,1,0:T(8,128)(2,1)S(1)}, bf16[16,256,256]{2,1,0:T(8,128)(2,1)S(1)}, bf16[3,16,256,32]...) custom-call(bf16[256,1024]{1,0:T(8,128)(2,1)} %wq.1, ...), custom_call_target="tpu_custom_call" | custom-call | tf_op jit(solution)/shard_map/gather/pallas_call | solution.py:334
  73.4 6.2 %merge.1 = (bf16[4096,1024]{1,0:T(8,128)(2,1)}, bf16[4096,256]{1,0:T(8,128)(2,1)}, bf16[4096,256]{1,0:T(8,128)(2,1)}, f32[1,1024]{1,0:T(1,128)}, f32[1,256]{1,0:...) custom-call(bf16[16,256,1024]{2,1,0:T(8,128)(2,1)S(1)} %get-tuple-element.22.rq, ...), custom_call_target="tpu_custom_call" | custom-call | tf_op jit(solution)/shard_map/merge/pallas_call | solution.py:361

commit v4 on v3

--- a/solution.py
+++ b/solution.py
@@ -10,14 +10,17 @@
 BLOCKS = SIDE * SIDE
 TP = 4
 RANK = 32
+PART = RANK // TP
 ROWS = 256
+HALF = ROWS // 2
 Q, KV = 1024, 256
 COLS = Q + 2 * KV
 AHEAD = 4
 SMALL_AT = AHEAD
 SMALL_LAG = AHEAD
 TP_AT = SMALL_AT + 4 * SMALL_LAG
-TP_WAIT = 10
+TP_WAIT = 8
+UNITS = 4
 DIRECTIONS = ((0, 1), (0, -1), (1, 1), (1, -1))
 
 BULK = [(0, 1, 1), (0, 1, 1), (0, 1, -1), (0, -1, 1), (0, -1, -1), (0, -1, -1)]
@@ -69,7 +72,7 @@
         now = {}
         for d in DIRECTIONS:
             can = [r for r in ready[d] if r[0] <= s - ahead]
-            can.sort(key=lambda r: (-depth(trees[r[1]], *r[4]), r[0], r[1]))
+            can.sort(key=lambda r: (r[4][1] != 0, min(2 * r[4][0], 7 - r[4][0]), -depth(trees[r[1]], *r[4]), r[0], r[1]))
             now[d] = can[:1]
             for r in now[d]:
                 ready[d].remove(r)
@@ -84,10 +87,53 @@
 N = len(STEPS)
 
 
+def half_blocks(steps, trees):
+    arrival = {}
+    for s, step in enumerate(steps):
+        for sent in step.values():
+            for c, _, _, to in sent:
+                key = (trees[c][0], *offsets(trees[c], *to))
+                arrival[key] = max(arrival.get(key, 0), s)
+    for half in range(2):
+        arrival[half, 0, 0] = -1
+    return sorted((at, *key) for key, at in arrival.items())
+
+
+LAST = SIDE // 2
+
+
+def merge_plan():
+    todo = [u for u in half_blocks(STEPS, BULK) if u[2:] != (LAST, LAST)]
+    out = {}
+    for s in range(TP_AT + TP_WAIT + 1, N + AHEAD):
+        now = [u for u in todo if u[0] + AHEAD <= s][:UNITS]
+        todo = todo[len(now) :]
+        out[s] = [u[1:] for u in now]
+    assert not todo
+    return out
+
+
+MERGES = merge_plan()
+
+
+def merge_half(raw, low, high2, inv, out, y, x, half, row):
+    rows = pl.ds(pl.multiple_of(half * HALF, HALF), HALF)
+    start = 0
+    for which, (w, o) in enumerate(zip(raw, out)):
+        left = low[:, y, x, which, :, rows].astype(jnp.float32).reshape(RANK, HALF).astype(jnp.bfloat16)
+        for j in range(w.shape[2] // KV):
+            cols, every = pl.ds(KV * j, KV), pl.ds(start + KV * j, KV)
+            fresh = w[y * SIDE + x, rows, cols].astype(jnp.float32) + lax.dot_general(
+                left, high2[:, every], (((0,), (0,)), ((), ())), preferred_element_type=jnp.float32
+            )
+            o[pl.ds(row, HALF), cols] = (fresh * inv[:, every]).astype(jnp.bfloat16)
+        start += w.shape[2]
+
+
 def gather_kernel(
     wq, wk, wv, lq, lk, lv, hq, hk, hv, train, step_in,
-    rq, rk, rv, left, high2, inv, column, norm_out,
-    own_low, high, norm_in, low, sums, norms, lines,
+    rq, rk, rv, oq, ok, ov, low, high2, inv, column, norm_out,
+    own_low, high, norm_in, sums, norms, lines,
     load_sem, send_sem, recv_sem, small_send, small_recv, tp_send, tp_recv,
 ):
     me = lax.axis_index("zero")
@@ -109,15 +155,15 @@
     for i in range(1, TP):
         pl.semaphore_signal(barrier, inc=1, device_id={"tp": (t + i) % TP}, device_id_type=MESH)
 
+    part = pl.ds(pl.multiple_of(t * PART, PART), PART)
     loads = [
         pltpu.make_async_copy(src, dst, load_sem.at[i])
-        for i, (src, dst) in enumerate(
-            (
-                (wq, rq.at[me]), (wk, rk.at[me]), (wv, rv.at[me]),
-                (lq, own_low.at[0]), (lk, own_low.at[1]), (lv, own_low.at[2]),
-                (hq, high.at[:, pl.ds(0, Q)]), (hk, high.at[:, pl.ds(Q, KV)]), (hv, high.at[:, pl.ds(Q + KV, KV)]),
-                (train, norm_in.at[0]), (step_in, norm_in.at[1]),
-            )
+        for src, dst, i in (
+            (wq, rq.at[me], 0), (wk, rk.at[me], 1), (wv, rv.at[me], 2),
+            (lq.at[part], low.at[t, y, x, 0], 3), (lk.at[part], low.at[t, y, x, 1], 3), (lv.at[part], low.at[t, y, x, 2], 3),
+            (lq, own_low.at[0], 4), (lk, own_low.at[1], 4), (lv, own_low.at[2], 4),
+            (hq, high.at[:, pl.ds(0, Q)], 5), (hk, high.at[:, pl.ds(Q, KV)], 5), (hv, high.at[:, pl.ds(Q + KV, KV)], 5),
+            (train, norm_in.at[0], 6), (step_in, norm_in.at[1], 6),
         )
     ]
     for load in loads:
@@ -137,13 +183,13 @@
         c, a, b, to = STEPS[s][d][0]
         ref = bulk_ref(c, *(to if opposite else (a, b)))
         return pltpu.make_async_remote_copy(
-            src_ref=ref, dst_ref=ref, send_sem=send_sem.at[k, s % AHEAD], recv_sem=recv_sem.at[k, s % (2 * AHEAD)],
+            src_ref=ref, dst_ref=ref, send_sem=send_sem.at[k], recv_sem=recv_sem.at[k, s % (2 * AHEAD)],
             device_id={"zero": towards[d]}, device_id_type=MESH,
         )
 
     def small_ref(c, where):
         if c < 2:
-            return low.at[(t, *where, pl.ds(16 * c, 16))]
+            return low.at[(t, *where, slice(None), slice(None), pl.ds(HALF * c, HALF))]
         return sums.at[(*where, slice(None), pl.ds(0, CUT) if c == 2 else pl.ds(CUT, COLS + 128 - CUT))]
 
     def small_copies(stage, received=False):
@@ -164,10 +210,9 @@
                         line = pl.ds(2 * n, 2)
                     return (line, at) if axis == 0 else (at, line)
 
-                slot = (0, 2, 3, 5)[stage] + (0 if stage == 1 else n)
                 ref = small_ref(c, piece(behind + received))
                 yield pltpu.make_async_remote_copy(
-                    src_ref=ref, dst_ref=ref, send_sem=small_send.at[c, slot], recv_sem=small_recv.at[c, slot],
+                    src_ref=ref, dst_ref=ref, send_sem=small_send.at[c, n], recv_sem=small_recv.at[c, n, stage % 2],
                     device_id={"zero": towards[axis, sign]}, device_id_type=MESH,
                 )
 
@@ -176,15 +221,20 @@
             ((low.at[owner], low.at[owner]), (sums.at[:, :, 0, pl.ds(COLS, 128)], norms.at[owner]))
         ):
             yield pltpu.make_async_remote_copy(
-                src_ref=src, dst_ref=dst, send_sem=tp_send.at[i - 1, j], recv_sem=tp_recv.at[i - 1, j],
+                src_ref=src, dst_ref=dst, send_sem=tp_send.at[j], recv_sem=tp_recv.at[j],
                 device_id={"tp": (t + i) % TP}, device_id_type=MESH,
+            )
+
+    def tp_waits():
+        for j, ref in enumerate((low.at[pl.ds(0, TP - 1)], norms.at[pl.ds(0, TP - 1)])):
+            yield pltpu.make_async_remote_copy(
+                src_ref=ref, dst_ref=ref, send_sem=tp_send.at[j], recv_sem=tp_recv.at[j],
+                device_id={"tp": (t + 1) % TP}, device_id_type=MESH,
             )
 
     def sends(s):
         for k, d in enumerate(DIRECTIONS):
             if s < N and STEPS[s][d]:
-                if s >= AHEAD:
-                    bulk_copy(s - AHEAD, k, False).wait_send()
                 bulk_copy(s, k, False).start()
 
     def receives(s):
@@ -194,20 +244,8 @@
 
     for s in range(AHEAD):
         sends(s)
-    for load in loads[3:]:
-        load.wait()
-
-    @pl.when(t == 0)
-    def _():
-        low[t, y, x] = own_low[0]
-
-    @pl.when(t == 1)
-    def _():
-        low[t, y, x] = own_low[1]
-
-    @pl.when(t >= 2)
-    def _():
-        low[t, y, x] = own_low[2]
+    for i, ref in ((3, low.at[t, y, x]), (4, own_low), (5, high), (6, norm_in)):
+        pltpu.make_async_copy(ref, ref, load_sem.at[i]).wait()
 
     high2[...] = high[...] * 2.0
 
@@ -236,13 +274,29 @@
             )
         norm_out[...] = lines[...].astype(jnp.bfloat16)
 
-    done = 0
+    def merges(units):
+        code = 0
+        for half, dy, dx in reversed(units):
+            code = 32 * code + (half * SIDE + dy) * SIDE + dx
+
+        def one(_, code):
+            half, dy, dx = code % 32 // BLOCKS, code % BLOCKS // SIDE, code % SIDE
+            by, bx = (y + SIDE - dy) % SIDE, (x + SIDE - dx) % SIDE
+            row = pl.multiple_of((by * SIDE + bx) * ROWS + half * HALF, HALF)
+            merge_half((rq, rk, rv), low, high2, inv, (oq, ok, ov), by, bx, half, row)
+            return code // 32
+
+        if units:
+            lax.fori_loop(0, len(units), one, jnp.int32(code))
+
     for s in range(AHEAD, N + AHEAD):
         receives(s - AHEAD)
         for stage in range(4):
             if s == SMALL_AT + (stage + 1) * SMALL_LAG:
                 for copy in small_copies(stage, True):
                     copy.wait_recv()
+                for copy in small_copies(stage):
+                    copy.wait_send()
         for stage in range(4):
             if s == SMALL_AT + stage * SMALL_LAG:
                 for copy in small_copies(stage):
@@ -253,33 +307,38 @@
                 for copy in tp_copies(t, i):
                     copy.start()
         if s == TP_AT + TP_WAIT:
-            for i in range(1, TP):
-                for copy in tp_copies((t + TP - i) % TP, i):
-                    copy.wait_recv()
+            for copy in tp_waits():
+                copy.wait_recv()
             scales()
-        if s > TP_AT + TP_WAIT:
-            while done < min(BLOCKS, 3 * (s - TP_AT - TP_WAIT)):
-                for which in range(3):
-                    left[which, done] = low[which, done // SIDE, done % SIDE].T
-                done += 1
-    assert done == BLOCKS
-    for i in range(1, TP):
-        for copy in tp_copies(t, i):
-            copy.wait_send()
-    for stage in range(4):
-        for copy in small_copies(stage):
-            copy.wait_send()
-    for s in range(N - AHEAD, N):
-        for k, d in enumerate(DIRECTIONS):
-            if STEPS[s][d]:
-                bulk_copy(s, k, False).wait_send()
+        merges(MERGES.get(s, []))
+    for copy in tp_waits():
+        copy.wait_send()
+    for k in range(len(DIRECTIONS)):
+        every = rq.at[pl.ds(0, BLOCKS - 1), pl.ds(0, 2 * N * ROWS // (BLOCKS - 1) // 16)]
+        pltpu.make_async_remote_copy(
+            src_ref=every, dst_ref=every, send_sem=send_sem.at[k], recv_sem=recv_sem.at[k, 0],
+            device_id={"zero": towards[DIRECTIONS[k]]}, device_id_type=MESH,
+        ).wait_send()
 
 
 def merge_kernel(
-    rq, rk, rv, left, high2, inv, column, norm,
+    rq, rk, rv, oq, ok, ov, low, high2, inv, column, norm,
     sq, sk, sv, cq, ck, cv, norm_out,
-    oq, ok, ov, out_sem, end_sem,
+    lq, lk, lv, out_sem, end_sem,
 ):
+    me = lax.axis_index("zero")
+    y, x = (me // SIDE + LAST) % SIDE, (me + LAST) % SIDE
+    last = y * SIDE + x
+    outs = ((oq, lq, sq), (ok, lk, sk), (ov, lv, sv))
+
+    def one(i, _):
+        b = (last + 1 + i) % BLOCKS
+        rows = pl.ds(pl.multiple_of(b * ROWS, ROWS), ROWS)
+        for i, (o, _, s) in enumerate(outs):
+            pltpu.make_async_copy(o.at[rows], s.at[rows], out_sem.at[i]).start()
+        return 0
+
+    lax.fori_loop(0, BLOCKS - 1, one, 0)
     ends = [
         pltpu.make_async_copy(src, dst, end_sem.at[i])
         for i, (src, dst) in enumerate(
@@ -293,26 +352,13 @@
     ]
     for copy in ends:
         copy.start()
-
-    parts = ((rq, 0, oq, sq, 0), (rk, 1, ok, sk, Q), (rv, 2, ov, sv, Q + KV))
-
-    def one(b, _):
-        place = pl.ds(pl.multiple_of(b * ROWS, ROWS), ROWS)
-        for i, (w, which, o, serve, start) in enumerate(parts):
-            rows = left[which, b]
-            for j in range(w.shape[2] // KV):
-                cols = pl.ds(KV * j, KV)
-                every = pl.ds(start + KV * j, KV)
-                fresh = w[b, :, cols].astype(jnp.float32) + jnp.dot(
-                    rows, high2[:, every], preferred_element_type=jnp.float32
-                )
-                o[place, cols] = (fresh * inv[:, every]).astype(jnp.bfloat16)
-            pltpu.make_async_copy(o.at[place], serve.at[place], out_sem.at[i]).start()
-        return 0
-
-    lax.fori_loop(0, BLOCKS, one, 0)
-    for i, (_, _, o, serve, _) in enumerate(parts):
-        pltpu.make_async_copy(o, serve, out_sem.at[i]).wait()
+    for half in range(2):
+        merge_half((rq, rk, rv), low, high2, inv, (lq, lk, lv), y, x, half, half * HALF)
+    rows = pl.ds(pl.multiple_of(last * ROWS, ROWS), ROWS)
+    for i, (_, o, s) in enumerate(outs):
+        pltpu.make_async_copy(o, s.at[rows], out_sem.at[i]).start()
+    for i, (o, _, s) in enumerate(outs):
+        pltpu.make_async_copy(o, s, out_sem.at[i]).wait()
     for copy in ends:
         copy.wait()
 
@@ -338,23 +384,25 @@
             pltpu.VMEM((BLOCKS, ROWS, Q), bf16),
             pltpu.VMEM((BLOCKS, ROWS, KV), bf16),
             pltpu.VMEM((BLOCKS, ROWS, KV), bf16),
-            pltpu.VMEM((3, BLOCKS, ROWS, RANK), bf16),
+            pltpu.VMEM((BLOCKS * ROWS, Q), bf16),
+            pltpu.VMEM((BLOCKS * ROWS, KV), bf16),
+            pltpu.VMEM((BLOCKS * ROWS, KV), bf16),
+            pltpu.VMEM((TP, SIDE, SIDE, 3, PART, ROWS), bf16),
             pltpu.VMEM((RANK, COLS), bf16),
             pltpu.VMEM((1, COLS), f32),
             pltpu.VMEM((1, COLS), f32),
             pltpu.VMEM((2 * BLOCKS, 128), bf16),
         ),
         in_specs=[hbm] * 11,
-        out_specs=[vmem] * 8,
+        out_specs=[vmem] * 11,
         scratch_shapes=[
             pltpu.VMEM((3, RANK, ROWS), bf16),
             pltpu.VMEM((RANK, COLS), bf16),
             pltpu.VMEM((2, 1, 64), f32),
-            pltpu.VMEM((TP, SIDE, SIDE, RANK, ROWS), bf16),
             pltpu.VMEM((SIDE, SIDE, 1, COLS + 128), f32),
             pltpu.VMEM((TP, SIDE, SIDE, 128), f32),
             pltpu.VMEM((2 * BLOCKS, 128), f32),
-            dma((11,)), dma((4, AHEAD)), dma((4, 2 * AHEAD)), dma((4, 7)), dma((4, 7)), dma((TP - 1, 2)), dma((TP - 1, 2)),
+            dma((7,)), dma((4,)), dma((4, 2 * AHEAD)), dma((4, 2)), dma((4, 2, 2)), dma((2,)), dma((2,)),
         ],
         compiler_params=pltpu.CompilerParams(collective_id=0, has_side_effects=True, vmem_limit_bytes=16 << 20),
     )(*(pltpu.with_memory_space_constraint(a, pltpu.HBM) for a in inputs))
@@ -370,16 +418,16 @@
             pltpu.HBM((1, KV), f32),
             pltpu.HBM((2 * BLOCKS, 128), bf16),
         ),
-        in_specs=[vmem] * 8,
+        in_specs=[vmem] * 11,
         out_specs=[hbm] * 7,
         scratch_shapes=[
-            pltpu.VMEM((BLOCKS * ROWS, Q), bf16),
-            pltpu.VMEM((BLOCKS * ROWS, KV), bf16),
-            pltpu.VMEM((BLOCKS * ROWS, KV), bf16),
+            pltpu.VMEM((ROWS, Q), bf16),
+            pltpu.VMEM((ROWS, KV), bf16),
+            pltpu.VMEM((ROWS, KV), bf16),
             dma((3,)),
             dma((4,)),
         ],
-        compiler_params=pltpu.CompilerParams(vmem_limit_bytes=24 << 20),
+        compiler_params=pltpu.CompilerParams(vmem_limit_bytes=16 << 20),
     )(*gathered)
     return sq, sk, sv, cq.reshape(Q), ck.reshape(KV), cv.reshape(KV), norm.reshape(BLOCKS * ROWS)
 

time: 79.9 us -> 77.3 us (0.967)
  Pallas kernels: 79.1 us -> 76.5 us
    pallas_call x1, Pallas kernels: 6.25 us -> 4.62 us  [on_device(): pl.pallas_call(merge_kernel, name='merge', out_shape=(pltpu.HBM((BLOCKS *...]
    pallas_call x1, Pallas kernels: 72.8 us -> 71.9 us  [on_device(): pl.pallas_call(gather_kernel, name='gather', out_shape=(pltpu.VMEM((BLOCK...]
where the time goes in v4:
time: 77.3 us; the launch traced here: 77.2 us
  Pallas kernels  76.5 us (99%)
    pallas_call x1, Pallas kernels, on_device(): pl.pallas_call(gather_kernel, name='gather', out_shape=(pltpu.VMEM((BLOCK...  71.9 us
    pallas_call x1, Pallas kernels, on_device(): pl.pallas_call(merge_kernel, name='merge', out_shape=(pltpu.HBM((BLOCKS *...  4.62 us

profile of v4, /device:TPU:32, one launch (start us, length us, event | category | flops | bytes accessed | tf_op | source)
XLA Modules:
  0.0 77.2 jit_solution(7173011783107831939)
XLA Ops:
  0.6 71.9 %gather.1 = (bf16[16,256,1024]{2,1,0:T(8,128)(2,1)S(1)}, bf16[16,256,256]{2,1,0:T(8,128)(2,1)S(1)}, bf16[16,256,256]{2,1,0:T(8,128)(2,1)S(1)}, bf16[4096,1024]{1...) custom-call(bf16[256,1024]{1,0:T(8,128)(2,1)} %wq.1, ...), custom_call_target="tpu_custom_call" | custom-call | tf_op jit(solution)/shard_map/gather/pallas_call | solution.py:380
  72.5 4.6 %merge.1 = (bf16[4096,1024]{1,0:T(8,128)(2,1)}, bf16[4096,256]{1,0:T(8,128)(2,1)}, bf16[4096,256]{1,0:T(8,128)(2,1)}, f32[1,1024]{1,0:T(1,128)}, f32[1,256]{1,0:...) custom-call(bf16[16,256,1024]{2,1,0:T(8,128)(2,1)S(1)} %get-tuple-element.25.rq, ...), custom_call_target="tpu_custom_call" | custom-call | tf_op jit(solution)/shard_map/merge/pallas_call | solution.py:409

commit v5 on v4

--- a/solution.py
+++ b/solution.py
@@ -16,9 +16,9 @@
 Q, KV = 1024, 256
 COLS = Q + 2 * KV
 AHEAD = 4
-SMALL_AT = AHEAD
 SMALL_LAG = AHEAD
-TP_AT = SMALL_AT + 4 * SMALL_LAG
+STAGE_AT = tuple(AHEAD + i * SMALL_LAG + (i > 1) for i in range(4))
+TP_AT = STAGE_AT[3] + SMALL_LAG
 TP_WAIT = 8
 UNITS = 4
 DIRECTIONS = ((0, 1), (0, -1), (1, 1), (1, -1))
@@ -27,7 +27,7 @@
 BULK = BULK + [(1, s1, s2) for _, s1, s2 in BULK]
 BULK_PLACE = [("q", 0), ("q", 1), ("k", 0), ("q", 2), ("v", 0), ("q", 3)]
 BULK_PLACE = BULK_PLACE + [("q", 4), ("q", 5), ("k", 1), ("q", 6), ("v", 1), ("q", 7)]
-SMALL = [0, 1, 0, 1]
+SMALL = [0, 1, 0, 1, 0]
 CUT = 768
 
 
@@ -133,7 +133,7 @@
 def gather_kernel(
     wq, wk, wv, lq, lk, lv, hq, hk, hv, train, step_in,
     rq, rk, rv, oq, ok, ov, low, high2, inv, column, norm_out,
-    own_low, high, norm_in, sums, norms, lines,
+    own_low, high, norm_in, sums, line_sums, norms, lines,
     load_sem, send_sem, recv_sem, small_send, small_recv, tp_send, tp_recv,
 ):
     me = lax.axis_index("zero")
@@ -190,31 +190,32 @@
     def small_ref(c, where):
         if c < 2:
             return low.at[(t, *where, slice(None), slice(None), pl.ds(HALF * c, HALF))]
-        return sums.at[(*where, slice(None), pl.ds(0, CUT) if c == 2 else pl.ds(CUT, COLS + 128 - CUT))]
+        return sums.at[(*where, slice(None), pl.ds(*((0, CUT), (CUT, COLS - CUT), (COLS, 128))[c - 2]))]
 
     def small_copies(stage, received=False):
         for c, first in enumerate(SMALL):
             axis = first if stage < 2 else 1 - first
+            summed = c in (2, 3) and stage >= 2
             for n, sign in enumerate((1, -1)):
-                if stage == 1 and (n == 0) != (c % 2 == 0):
+                if (stage == 1 or stage == 3 and summed) and (n == 0) != (c % 2 == 0):
                     continue
-                behind = 0 if stage % 2 == 0 else 1
-
-                def piece(back):
-                    at = (x, y)[axis]
-                    at = (at + 2 * SIDE - sign * back) % SIDE
-                    if stage < 2:
-                        return (y, at) if axis == 0 else (at, x)
-                    line = slice(None)
-                    if stage == 3:
-                        line = pl.ds(2 * n, 2)
-                    return (line, at) if axis == 0 else (at, line)
-
-                ref = small_ref(c, piece(behind + received))
+                at = ((x, y)[axis] + 2 * SIDE - sign * (stage % 2 + received)) % SIDE
+                if summed:
+                    ref = line_sums.at[c - 2, at]
+                else:
+                    across = (y, x)[axis] if stage < 2 else slice(None) if stage == 2 else pl.ds(2 * n, 2)
+                    ref = small_ref(c, (across, at) if axis == 0 else (at, across))
                 yield pltpu.make_async_remote_copy(
                     src_ref=ref, dst_ref=ref, send_sem=small_send.at[c, n], recv_sem=small_recv.at[c, n, stage % 2],
                     device_id={"zero": towards[axis, sign]}, device_id_type=MESH,
                 )
+
+    def line_totals():
+        for c, here in ((2, y), (3, x)):
+            total = small_ref(c, (y, 0) if c == 2 else (0, x))[...]
+            for i in range(1, SIDE):
+                total = total + small_ref(c, (y, i) if c == 2 else (i, x))[...]
+            line_sums[c - 2, here] = total
 
     def tp_copies(owner, i):
         for j, (src, dst) in enumerate(
@@ -260,12 +261,13 @@
     sums[y, x, :, pl.ds(COLS, 128)] = jnp.concatenate([norm_in[0] + norm_in[1]] * 2, axis=1)
 
     def scales():
-        total = sums[0, 0, :, pl.ds(0, COLS)]
-        for b in range(1, BLOCKS):
-            total = total + sums[b // SIDE, b % SIDE, :, pl.ds(0, COLS)]
-        scale = jnp.sqrt(total)
-        column[...] = scale
-        inv[...] = 1.0 / scale
+        for c, start in ((0, 0), (1, CUT)):
+            total = line_sums[c, 0]
+            for i in range(1, SIDE):
+                total = total + line_sums[c, i]
+            scale = jnp.sqrt(total)
+            column[:, pl.ds(start, CUT)] = scale
+            inv[:, pl.ds(start, CUT)] = 1.0 / scale
         norms[t] = sums[:, :, 0, pl.ds(COLS, 128)]
         lane = lax.broadcasted_iota(jnp.int32, (BLOCKS, 128), 1)
         for p in range(2):
@@ -292,13 +294,15 @@
     for s in range(AHEAD, N + AHEAD):
         receives(s - AHEAD)
         for stage in range(4):
-            if s == SMALL_AT + (stage + 1) * SMALL_LAG:
+            if s == STAGE_AT[stage] + SMALL_LAG:
                 for copy in small_copies(stage, True):
                     copy.wait_recv()
                 for copy in small_copies(stage):
                     copy.wait_send()
+                if stage == 1:
+                    line_totals()
         for stage in range(4):
-            if s == SMALL_AT + stage * SMALL_LAG:
+            if s == STAGE_AT[stage]:
                 for copy in small_copies(stage):
                     copy.start()
         sends(s)
@@ -333,9 +337,10 @@
 
     def one(i, _):
         b = (last + 1 + i) % BLOCKS
-        rows = pl.ds(pl.multiple_of(b * ROWS, ROWS), ROWS)
-        for i, (o, _, s) in enumerate(outs):
-            pltpu.make_async_copy(o.at[rows], s.at[rows], out_sem.at[i]).start()
+        for half in range(2):
+            rows = pl.ds(pl.multiple_of(b * ROWS + half * HALF, HALF), HALF)
+            for i, (o, _, s) in enumerate(outs):
+                pltpu.make_async_copy(o.at[rows], s.at[rows], out_sem.at[i]).start()
         return 0
 
     lax.fori_loop(0, BLOCKS - 1, one, 0)
@@ -400,9 +405,10 @@
             pltpu.VMEM((RANK, COLS), bf16),
             pltpu.VMEM((2, 1, 64), f32),
             pltpu.VMEM((SIDE, SIDE, 1, COLS + 128), f32),
+            pltpu.VMEM((2, SIDE, 1, CUT), f32),
             pltpu.VMEM((TP, SIDE, SIDE, 128), f32),
             pltpu.VMEM((2 * BLOCKS, 128), f32),
-            dma((7,)), dma((4,)), dma((4, 2 * AHEAD)), dma((4, 2)), dma((4, 2, 2)), dma((2,)), dma((2,)),
+            dma((7,)), dma((4,)), dma((4, 2 * AHEAD)), dma((5, 2)), dma((5, 2, 2)), dma((2,)), dma((2,)),
         ],
         compiler_params=pltpu.CompilerParams(collective_id=0, has_side_effects=True, vmem_limit_bytes=16 << 20),
     )(*(pltpu.with_memory_space_constraint(a, pltpu.HBM) for a in inputs))

time: 77.3 us -> 76.9 us (level)
  no operation moved by 1% of the time
where the time goes in v5:
time: 76.9 us; the launch traced here: 76.8 us
  Pallas kernels  76.2 us (99%)
    pallas_call x1, Pallas kernels, on_device(): pl.pallas_call(gather_kernel, name='gather', out_shape=(pltpu.VMEM((BLOCK...  71.6 us
    pallas_call x1, Pallas kernels, on_device(): pl.pallas_call(merge_kernel, name='merge', out_shape=(pltpu.HBM((BLOCKS *...  4.61 us

profile of v5, /device:TPU:32, one launch (start us, length us, event | category | flops | bytes accessed | tf_op | source)
XLA Modules:
  0.0 76.8 jit_solution(8939640946836180637)
XLA Ops:
  0.6 71.6 %gather.1 = (bf16[16,256,1024]{2,1,0:T(8,128)(2,1)S(1)}, bf16[16,256,256]{2,1,0:T(8,128)(2,1)S(1)}, bf16[16,256,256]{2,1,0:T(8,128)(2,1)S(1)}, bf16[4096,1024]{1...) custom-call(bf16[256,1024]{1,0:T(8,128)(2,1)} %wq.1, ...), custom_call_target="tpu_custom_call" | custom-call | tf_op jit(solution)/shard_map/gather/pallas_call | solution.py:385
  72.2 4.6 %merge.1 = (bf16[4096,1024]{1,0:T(8,128)(2,1)}, bf16[4096,256]{1,0:T(8,128)(2,1)}, bf16[4096,256]{1,0:T(8,128)(2,1)}, f32[1,1024]{1,0:T(1,128)}, f32[1,256]{1,0:...) custom-call(bf16[16,256,1024]{2,1,0:T(8,128)(2,1)S(1)} %get-tuple-element.25.rq, ...), custom_call_target="tpu_custom_call" | custom-call | tf_op jit(solution)/shard_map/merge/pallas_call | solution.py:415
